TPU v7x, 32 devices: a whole 2x2x4 slice. The times are simulated.
32 devices in a mesh: tile: 8 (over z, y), lev: 4 (over x, core).
Axes of the slice: x: 2, y: 2, z: 4, core: 2. Of those that a mesh axis runs over, the one named last changes fastest.
Arguments:
- ensemble: bfloat16 [80, 32, 4096], P(None, 'lev', 'tile')
- pair_first: int32 [32768], P('tile'), may hold values from 0 to 511
- pair_second: int32 [32768], P('tile'), may hold values from 0 to 1023
- pair_bin: int32 [32768], P('tile'), may hold values from 0 to 63, as said below
Outputs:
- level_variance: float32 [32], P('lev')
- bin_corr: float32 [32, 64], P('lev', 'tile')
- bin_avg: float32 [64], P('tile')
Inputs may be any that keep to these rules, and one draw needn't show every extreme that they name: `pair_bin`: some bins receive no pair; which ones changes with the draw.
All inputs are finite; a program needn't handle non-finite values.
Results may differ from a plain program's by a relative error of at most 0.0017.
Values may be sent and summed in bfloat16 or wider, within the bound.
A program may use at most 64 MiB of HBM per device.

v0:
```python
import jax
import jax.numpy as jnp
from jax import lax
from jax.sharding import PartitionSpec as P

BIN_DEV = 8


def from_behind(block, axis, distance):
    devices = range(lax.axis_size(axis))
    route = [((i - distance) % len(devices), i) for i in devices]
    return lax.ppermute(block, axis, route)


def local(ensemble, pair_first, pair_second, pair_bin):
    members = ensemble.shape[0]
    lev_rows = ensemble.shape[1]
    col_rows = ensemble.shape[2]
    ntile = lax.axis_size("tile")
    values = ensemble.astype(jnp.float32)
    pert = (values - jnp.mean(values, axis=0, keepdims=True)).astype(jnp.bfloat16)
    own_squares = jnp.sum(jnp.square(pert.astype(jnp.float32)), axis=(0, 2))
    columns = jnp.transpose(pert, (2, 0, 1)).reshape(col_rows, members * lev_rows)
    following = from_behind(columns, "tile", -1)
    extended = jnp.concatenate([columns, following], axis=0)
    total_bins = BIN_DEV * ntile
    pair_rows = pair_first.shape[0]
    block = min(2048, pair_rows)
    blocks = pair_rows // block
    firsts = pair_first.reshape(blocks, block)
    seconds = pair_second.reshape(blocks, block)
    bins = pair_bin.reshape(blocks, block)
    bin_ids = jnp.arange(total_bins, dtype=jnp.int32)

    def accumulate(carry, items):
        sums, counts = carry
        first, second, where = items
        left = (
            jnp.take(extended, first, axis=0).astype(jnp.float32).reshape(block, members, lev_rows)
        )
        right = (
            jnp.take(extended, second, axis=0).astype(jnp.float32).reshape(block, members, lev_rows)
        )
        cov = jnp.sum(left * right, axis=1) / (members - 1)
        spread_left = jnp.sqrt(jnp.sum(left * left, axis=1) / (members - 1) + 1e-06)
        spread_right = jnp.sqrt(jnp.sum(right * right, axis=1) / (members - 1) + 1e-06)
        corr = cov / (spread_left * spread_right)
        onehot = (where[:, None] == bin_ids[None, :]).astype(jnp.float32)
        sums = sums + lax.dot_general(
            corr, onehot, (((0,), (0,)), ((), ())), precision=lax.Precision.HIGHEST
        )
        counts = counts + jnp.sum(onehot, axis=0)
        return ((sums, counts), None)

    start_carry = (
        jnp.zeros((lev_rows, total_bins), jnp.float32),
        jnp.zeros((total_bins,), jnp.float32),
    )
    (sums, counts), unused = lax.scan(accumulate, start_carry, (firsts, seconds, bins))
    all_sums, all_counts, squares = lax.psum((sums, counts, own_squares), "tile")
    offset = lax.axis_index("tile") * BIN_DEV
    bin_sum = lax.dynamic_slice_in_dim(all_sums, offset, BIN_DEV, 1)
    bin_count = lax.dynamic_slice_in_dim(all_counts, offset, BIN_DEV, 0)
    level_variance = squares / ((members - 1) * col_rows * ntile)
    bin_corr = bin_sum / jnp.maximum(bin_count, 1.0)[None, :]
    weighted, weight_total = lax.psum(
        (jnp.sum(level_variance[:, None] * bin_corr, axis=0), jnp.sum(level_variance)), "lev"
    )
    bin_avg = weighted / weight_total
    return (level_variance, bin_corr, bin_avg)


def solution(mesh):
    in_specs = (P(None, "lev", "tile"), P("tile"), P("tile"), P("tile"))
    out_specs = (P("lev"), P("lev", "tile"), P("tile"))
    return jax.shard_map(local, mesh=mesh, in_specs=in_specs, out_specs=out_specs, check_vma=False)
```

profile of v0, /device:TPU:0, one launch (start us, length us, event | category | flops | bytes accessed | tf_op | source)
XLA Modules:
  0.0 163.2 jit_solution(2314394620306730304)
XLA Ops:
  0.6 1.2 convert_reduce_fusion
  1.9 2.1 %fusion.13 = (bf16[512,640]{0,1:T(8,128)(2,1)S(1)}, f32[8]{0:T(128)}) fusion(f32[8,512]{1,0:T(8,128)S(1)} %broadcast_multiply_fusion, bf16[80,8,512]{2,1,0:T(8,128)(2,1)} %param.8), kind=kLoop, calls=%fused_computation.37 | loop fusion | flops 1966072 | bytes 1327136 | tf_op jit(solution)/shard_map/reshape | solution.py:23
  3.9 6.0 %collective-permute-start = (bf16[512,640]{0,1:T(8,128)(2,1)S(1)}, bf16[512,640]{0,1:T(8,128)(2,1)S(1)}, u32[]{:S(2)}, u32[]{:S(2)}) collective-permute-start(bf16[512,640]{0,1:T(8,128)(2,1)S(1)} %get-tuple-element.124), channel_id=1, source_target_pairs={{4,0},{8,4},{12,8},{16,12},{20,16},{24,20},{28,24},{0,28},{5,1},{9... | collective-permute-start | bytes 1966088 | tf_op jit(solution)/shard_map/ppermute | solution.py:12
  9.9 0.7 reshape.37
  10.7 0.7 reshape.39
  11.4 0.7 reshape.40
  12.1 11.8 %collective-permute-done = bf16[512,640]{0,1:T(8,128)(2,1)S(1)} collective-permute-done((bf16[512,640]{0,1:T(8,128)(2,1)S(1)}, bf16[512,640]{0,1:T(8,128)(2,1)S(1)}, u32[]{:S(2)}, u32[]{:S(2)}) %collective-permute-start) | collective-permute-done | bytes 655392 | tf_op jit(solution)/shard_map/ppermute | solution.py:12
  24.1 0.7 copy.19
  24.9 106.9 %while.13 = (s32[]{:T(128)}, f32[8,64]{1,0:T(8,128)S(1)}, f32[64]{0:T(128)S(1)}, s32[2,2048]{1,0:T(2,128)S(1)}, bf16[1024,640]{1,0:T(8,128)(2,1)S(1)}, /*index=5...) while((s32[]{:T(128)}, f32[8,64]{1,0:T(8,128)S(1)}, f32[64]{0:T(128)S(1)}, ...), condition=%wide.region_8.10_spmd.clone, body=%wide.region_3.9_spmd.clone.sunk | while | flops 26321988 | bytes 79180904 | solution.py:59
  24.9 9.3 %gather_fusion.1 = bf16[2048,640]{1,0:T(8,128)(2,1)} fusion(bf16[1024,640]{1,0:T(8,128)(2,1)S(1)} %get-tuple-element.202, s32[2048]{0:T(1024)S(1)} %fusion.20), kind=kCustom, calls=%fused_computation.1.clone.clone.1 | custom fusion | bytes 5251072 | tf_op jit(solution)/shard_map/while/body/eval_jaxpr/jit(_take)/gather | solution.py:42
  34.3 9.3 %gather_fusion = bf16[2048,640]{1,0:T(8,128)(2,1)} fusion(bf16[1024,640]{1,0:T(8,128)(2,1)S(1)} %get-tuple-element.202, s32[2048]{0:T(1024)S(1)} %fusion.19), kind=kCustom, calls=%fused_computation.clone.clone.1 | custom fusion | bytes 5251072 | tf_op jit(solution)/shard_map/while/body/eval_jaxpr/jit(_take)/gather | solution.py:39
  43.6 8.0 %convert_multiply_fusion.4 = (f32[2048,640]{1,0:T(8,128)}, f32[2048,640]{1,0:T(8,128)}, f32[2048,640]{1,0:T(8,128)}) fusion(bf16[2048,640]{1,0:T(8,128)(2,1)} %gather_fusion, pred[2048]{0:T(1024)(128)(4,1)S(1)} %compare_and_fusion.4, bf16[2048,640]{1,0:T(8,128)(2,1)} %gather_fusion.1, pred[2048]{0:T(1024)(128)(4,1)S(1)} %compare_and_fusion.5), kind=kLoop, calls=%fused_computation.4.clone.1 | loop fusion | flops 9175040 | bytes 20975616 | tf_op jit(solution)/shard_map/while/body/eval_jaxpr/mul | solution.py:44
  51.6 5.9 %copy.23 = f32[2048,640]{0,1:T(8,128)} copy(f32[2048,640]{1,0:T(8,128)} %get-tuple-element.177) | data formatting | bytes 10485760 | tf_op jit(solution)/shard_map/while/body/eval_jaxpr/mul | solution.py:46
  57.5 2.8 %bitcast_reduce_fusion.6 = f32[2048,8]{0,1:T(8,128)S(1)} fusion(f32[2048,640]{0,1:T(8,128)} %copy.23), kind=kLoop, calls=%fused_computation.6.clone.1 | loop fusion | flops 1294336 | bytes 5308416 | tf_op jit(solution)/shard_map/while/body/eval_jaxpr/reduce_sum | solution.py:46
  60.2 5.9 %copy.24 = f32[2048,640]{0,1:T(8,128)} copy(f32[2048,640]{1,0:T(8,128)} %get-tuple-element.178) | data formatting | bytes 10485760 | tf_op jit(solution)/shard_map/while/body/eval_jaxpr/mul | solution.py:45
  66.2 2.8 %bitcast_reduce_fusion.7 = f32[2048,8]{0,1:T(8,128)S(1)} fusion(f32[2048,640]{0,1:T(8,128)} %copy.24), kind=kLoop, calls=%fused_computation.7.clone.1 | loop fusion | flops 1294336 | bytes 5308416 | tf_op jit(solution)/shard_map/while/body/eval_jaxpr/reduce_sum | solution.py:45
  68.9 6.0 %copy.25 = f32[2048,640]{0,1:T(8,128)} copy(f32[2048,640]{1,0:T(8,128)} %get-tuple-element.179) | data formatting | bytes 10485760 | tf_op jit(solution)/shard_map/while/body/eval_jaxpr/mul | solution.py:44
  75.0 2.8 %bitcast_reduce_fusion.8 = f32[2048,8]{0,1:T(8,128)S(1)} fusion(f32[2048,640]{0,1:T(8,128)} %copy.25), kind=kLoop, calls=%fused_computation.8.clone.1 | loop fusion | flops 1294336 | bytes 5308416 | tf_op jit(solution)/shard_map/while/body/eval_jaxpr/reduce_sum | solution.py:44
  78.4 9.3 %gather_fusion.1 = bf16[2048,640]{1,0:T(8,128)(2,1)} fusion(bf16[1024,640]{1,0:T(8,128)(2,1)S(1)} %get-tuple-element.202, s32[2048]{0:T(1024)S(1)} %fusion.20), kind=kCustom, calls=%fused_computation.1.clone.clone.1 | custom fusion | bytes 5251072 | tf_op jit(solution)/shard_map/while/body/eval_jaxpr/jit(_take)/gather | solution.py:42
  87.7 9.3 %gather_fusion = bf16[2048,640]{1,0:T(8,128)(2,1)} fusion(bf16[1024,640]{1,0:T(8,128)(2,1)S(1)} %get-tuple-element.202, s32[2048]{0:T(1024)S(1)} %fusion.19), kind=kCustom, calls=%fused_computation.clone.clone.1 | custom fusion | bytes 5251072 | tf_op jit(solution)/shard_map/while/body/eval_jaxpr/jit(_take)/gather | solution.py:39
  97.0 8.0 %convert_multiply_fusion.4 = (f32[2048,640]{1,0:T(8,128)}, f32[2048,640]{1,0:T(8,128)}, f32[2048,640]{1,0:T(8,128)}) fusion(bf16[2048,640]{1,0:T(8,128)(2,1)} %gather_fusion, pred[2048]{0:T(1024)(128)(4,1)S(1)} %compare_and_fusion.4, bf16[2048,640]{1,0:T(8,128)(2,1)} %gather_fusion.1, pred[2048]{0:T(1024)(128)(4,1)S(1)} %compare_and_fusion.5), kind=kLoop, calls=%fused_computation.4.clone.1 | loop fusion | flops 9175040 | bytes 20975616 | tf_op jit(solution)/shard_map/while/body/eval_jaxpr/mul | solution.py:44
  105.0 5.9 %copy.23 = f32[2048,640]{0,1:T(8,128)} copy(f32[2048,640]{1,0:T(8,128)} %get-tuple-element.177) | data formatting | bytes 10485760 | tf_op jit(solution)/shard_map/while/body/eval_jaxpr/mul | solution.py:46
  110.9 2.8 %bitcast_reduce_fusion.6 = f32[2048,8]{0,1:T(8,128)S(1)} fusion(f32[2048,640]{0,1:T(8,128)} %copy.23), kind=kLoop, calls=%fused_computation.6.clone.1 | loop fusion | flops 1294336 | bytes 5308416 | tf_op jit(solution)/shard_map/while/body/eval_jaxpr/reduce_sum | solution.py:46
  113.7 5.9 %copy.24 = f32[2048,640]{0,1:T(8,128)} copy(f32[2048,640]{1,0:T(8,128)} %get-tuple-element.178) | data formatting | bytes 10485760 | tf_op jit(solution)/shard_map/while/body/eval_jaxpr/mul | solution.py:45
  119.6 2.8 %bitcast_reduce_fusion.7 = f32[2048,8]{0,1:T(8,128)S(1)} fusion(f32[2048,640]{0,1:T(8,128)} %copy.24), kind=kLoop, calls=%fused_computation.7.clone.1 | loop fusion | flops 1294336 | bytes 5308416 | tf_op jit(solution)/shard_map/while/body/eval_jaxpr/reduce_sum | solution.py:45
  122.4 6.0 %copy.25 = f32[2048,640]{0,1:T(8,128)} copy(f32[2048,640]{1,0:T(8,128)} %get-tuple-element.179) | data formatting | bytes 10485760 | tf_op jit(solution)/shard_map/while/body/eval_jaxpr/mul | solution.py:44
  128.4 2.8 %bitcast_reduce_fusion.8 = f32[2048,8]{0,1:T(8,128)S(1)} fusion(f32[2048,640]{0,1:T(8,128)} %copy.25), kind=kLoop, calls=%fused_computation.8.clone.1 | loop fusion | flops 1294336 | bytes 5308416 | tf_op jit(solution)/shard_map/while/body/eval_jaxpr/reduce_sum | solution.py:44
  131.8 22.5 %all-reduce = (f32[8]{0:T(128)S(1)}, f32[8,64]{1,0:T(8,128)S(1)}, f32[64]{0:T(128)S(1)}) all-reduce(f32[8]{0:T(128)S(1)} %copy-done, f32[8,64]{1,0:T(8,128)S(1)} %get-tuple-element.47, f32[64]{0:T(128)S(1)} %get-tuple-element.48), channel_id=1, replica_groups=mesh['tile'=8,'lev'=4] {'tile'}, use_global_device_ids=true, to_apply=%region_2.3 | all-reduce | flops 584 | bytes 4672 | tf_op jit(solution)/shard_map/psum | solution.py:60
  154.3 0.6 fusion.14
  154.9 0.7 multiply_reduce_fusion.1
  155.6 6.3 %all-reduce.1 = (f32[8]{0:T(128)S(1)}, f32[]{:T(128)}) all-reduce(f32[8]{0:T(128)S(1)} %get-tuple-element.117, f32[]{:T(128)} %get-tuple-element.115), channel_id=1, replica_groups=mesh['tile'=8,'lev'=4] {'lev'}, use_global_device_ids=true, to_apply=%region_12.14 | all-reduce | flops 9 | bytes 72 | tf_op jit(solution)/shard_map/psum | solution.py:66
  162.0 1.2 broadcast_divide_fusion
  (26 shorter events, 1.4 us)
Async XLA Ops:
  3.9 20.0 %collective-permute-start = (bf16[512,640]{0,1:T(8,128)(2,1)S(1)}, bf16[512,640]{0,1:T(8,128)(2,1)S(1)}, u32[]{:S(2)}, u32[]{:S(2)}) collective-permute-start(bf16[512,640]{0,1:T(8,128)(2,1)S(1)} %get-tuple-element.124), channel_id=1, source_target_pairs={{4,0},{8,4},{12,8},{16,12},{20,16},{24,20},{28,24},{0,28},{5,1},{9... | collective-permute-start | bytes 1966088 | tf_op jit(solution)/shard_map/ppermute | solution.py:12
  24.8 106.9 %copy-start = (f32[8]{0:T(128)S(1)}, f32[8]{0:T(128)}, u32[]{:S(2)}) copy-start(f32[8]{0:T(128)} %get-tuple-element.125) | copy-start | bytes 100
  154.9 8.2 %copy-start.1 = (f32[8]{0:T(128)}, f32[8]{0:T(128)S(1)}, u32[]{:S(2)}) copy-start(f32[8]{0:T(128)S(1)} %get-tuple-element.116) | copy-start | bytes 100
where the time goes:
time: 164 us; the launch traced here: 163 us
  local copies, waits for them, and re-layouts  76 us (46%)
  other arithmetic  38.9 us (24%)
  blocking collectives  28.9 us (18%)
  waiting for transfers between devices  11.8 us (7%)
  starting transfers between devices  6.03 us (4%)
    psum x1, blocking collectives, local(): lax.psum((sums, counts, own_squares), 'tile')  22.5 us
    gather x2, local copies, waits for them, and re-layouts, accumulate(): jnp.take(extended, second, axis=0).astype(jnp.float32)  18.7 us
    gather x2, local copies, waits for them, and re-layouts, accumulate(): jnp.take(extended, first, axis=0).astype(jnp.float32)  18.6 us
    mul x2, other arithmetic, accumulate(): cov = jnp.sum(left * right, axis=1) / (members - 1)  15.9 us
    mul x2, local copies, waits for them, and re-layouts, accumulate(): cov = jnp.sum(left * right, axis=1) / (members - 1)  12.1 us
    mul x2, local copies, waits for them, and re-layouts, accumulate(): right * right  11.9 us
    mul x2, local copies, waits for them, and re-layouts, accumulate(): spread_left = jnp.sqrt(jnp.sum(left * left, axis=1) / (members - 1) + 1e-06)  11.8 us
    ppermute x1, waiting for transfers between devices, from_behind(): return lax.ppermute(block, axis, route)  11.8 us
  transfers between devices with their start and end apart: 1, of which 1 were waited for; matrix products, arithmetic and copies ran while one was open for 1% of the time, Pallas kernels for 0%

commit v1 on v0

v1 whole, which is shorter than its diff:
```python
import functools

import jax
import jax.numpy as jnp
from jax import lax
from jax.experimental import pallas as pl
from jax.experimental.pallas import tpu as pltpu
from jax.sharding import PartitionSpec as P

BIN_DEV = 8
LANES = 128
PAIR_CHUNK = 512
HALO_CHUNKS = 2


def pieces3(x):
    a = x.astype(jnp.bfloat16).astype(jnp.float32)
    r = x - a
    b = r.astype(jnp.bfloat16).astype(jnp.float32)
    return a, b, r - b


def onehot(rows, base, count):
    ids = lax.broadcasted_iota(jnp.int32, (count, LANES), 0) + base
    parts = [jnp.where(ids == r, 1.0, 0.0) for r in rows]
    return jnp.concatenate(parts, axis=1).astype(jnp.bfloat16)


def perturb(raw, out, squares, width):
    members, lev = raw.shape[0], raw.shape[1]
    rows = members * lev
    for c in range(0, width, LANES):
        cs = pl.ds(c, LANES)
        x = raw[:, :, cs].astype(jnp.float32)
        mean = jnp.sum(x, axis=0) / members
        pert = (x - mean[None]).astype(jnp.bfloat16).astype(jnp.float32)
        sq = jnp.sum(pert * pert, axis=0)
        out[pl.ds(0, rows), cs] = pert.reshape(rows, LANES).astype(jnp.bfloat16)
        inv = 1.0 / jnp.sqrt(sq / (members - 1) + 1e-06)
        hi = inv.astype(jnp.bfloat16).astype(jnp.float32)
        out[pl.ds(rows, 2 * lev), cs] = jnp.concatenate([hi, inv - hi], axis=0).astype(jnp.bfloat16)
        if squares is not None:
            squares[:, cs] = sq


def kernel(
    ntile, nlev, ens, first_in, second_in, bin_in, lv_out, corr_out, avg_out,
    raw, halo, first, second, bins, own, nxt, squares, left_buf, cov_buf, ia_buf, ib_buf,
    bacc, sbuf, rbuf, lsend, lrecv,
    load_sem, halo_send, halo_recv, t_send, t_recv, l_send, l_recv,
):
    members, lev, cols = ens.shape
    rows = members * lev
    half = cols // HALO_CHUNKS
    total_bins = BIN_DEV * ntile
    chunks = left_buf.shape[0]
    groups = PAIR_CHUNK // LANES
    me = lax.axis_index("tile")
    my_lev = lax.axis_index("lev")

    barrier = pltpu.get_barrier_semaphore()
    for d in range(1, ntile):
        pl.semaphore_signal(
            barrier, inc=1, device_id=(lax.rem(me + d, ntile), my_lev),
            device_id_type=pl.DeviceIdType.MESH,
        )
    for d in range(1, nlev):
        pl.semaphore_signal(
            barrier, inc=1, device_id=(me, lax.rem(my_lev + d, nlev)),
            device_id_type=pl.DeviceIdType.MESH,
        )
    loads = [
        pltpu.make_async_copy(s, d, load_sem.at[i])
        for i, (s, d) in enumerate(
            ((ens, raw), (first_in, first), (second_in, second), (bin_in, bins))
        )
    ]
    for c in loads:
        c.start()
    loads[0].wait()
    pl.semaphore_wait(barrier, ntile - 1 + nlev - 1)
    prev = lax.rem(me + ntile - 1, ntile)
    halos = [
        pltpu.make_async_remote_copy(
            src_ref=raw.at[:, :, pl.ds(h * half, half)],
            dst_ref=halo.at[h],
            send_sem=halo_send.at[h],
            recv_sem=halo_recv.at[h],
            device_id=(prev, my_lev),
            device_id_type=pl.DeviceIdType.MESH,
        )
        for h in range(HALO_CHUNKS)
    ]
    for c in halos:
        c.start()
    for c in loads[1:]:
        c.wait()

    perturb(raw, own, squares, cols)

    def index_rows(ref, j):
        return [ref[pl.ds(j * groups + i, 1), :] for i in range(groups)]

    def product(a, b):
        return jnp.sum((a * b).reshape(members, lev, PAIR_CHUNK), axis=0)

    def own_step(j, carry):
        x = own[...]
        left = jnp.dot(x, onehot(index_rows(first, j), 0, cols), preferred_element_type=jnp.float32)
        left_buf[j] = left[:rows]
        right = jnp.dot(x, onehot(index_rows(second, j), 0, cols), preferred_element_type=jnp.float32)
        cov_buf[j] = product(left_buf[j], right[:rows])
        ia_buf[j] = left[rows:rows + lev] + left[rows + lev:]
        ib_buf[j] = right[rows:rows + lev] + right[rows + lev:]
        return carry

    lax.fori_loop(0, chunks, own_step, 0)
    bacc[...] = jnp.zeros_like(bacc)

    for h in range(HALO_CHUNKS):
        halos[h].wait_recv()
        perturb(halo.at[h], nxt.at[h], None, half)

        def next_step(j, carry):
            oh = onehot(index_rows(second, j), cols + h * half, half)
            right = jnp.dot(nxt[h], oh, preferred_element_type=jnp.float32)
            cov = cov_buf[j] + product(left_buf[j], right[:rows])
            ib = ib_buf[j] + right[rows:rows + lev] + right[rows + lev:]
            if h < HALO_CHUNKS - 1:
                cov_buf[j] = cov
                ib_buf[j] = ib
            else:
                corr = cov * ia_buf[j] * ib / (members - 1)
                parts = jnp.concatenate(
                    [*pieces3(corr), jnp.ones_like(corr),
                     jnp.zeros((LANES - 4 * lev, PAIR_CHUNK), jnp.float32)], axis=0
                ).astype(jnp.bfloat16)
                oh = onehot(index_rows(bins, j), 0, total_bins)
                bacc[...] += lax.dot_general(
                    oh, parts, (((1,), (1,)), ((), ())), preferred_element_type=jnp.float32
                )
            return carry

        lax.fori_loop(0, chunks, next_step, 0)

    sq_parts = jnp.concatenate(
        [jnp.zeros((4 * lev, cols), jnp.float32), *pieces3(squares[...]),
         jnp.zeros((LANES - 7 * lev, cols), jnp.float32)], axis=0
    ).astype(jnp.bfloat16)
    sq_row = lax.dot_general(
        jnp.ones((16, cols), jnp.bfloat16), sq_parts, (((1,), (1,)), ((), ())),
        preferred_element_type=jnp.float32,
    )[:BIN_DEV]
    for t in range(ntile):
        sbuf[t] = bacc[pl.ds(t * BIN_DEV, BIN_DEV), :] + sq_row
    rbuf[me] = sbuf[me]

    def t_copy(d):
        peer = lax.rem(me + d, ntile)
        return pltpu.make_async_remote_copy(
            src_ref=sbuf.at[peer], dst_ref=rbuf.at[me],
            send_sem=t_send.at[d], recv_sem=t_recv.at[me],
            device_id=(peer, my_lev), device_id_type=pl.DeviceIdType.MESH,
        )

    for d in range(1, ntile):
        t_copy(d).start()
    for d in range(1, ntile):
        src = lax.rem(me + d, ntile)
        pltpu.make_async_copy(rbuf.at[src], rbuf.at[src], t_recv.at[src]).wait()
    tot = rbuf[0]
    for t in range(1, ntile):
        tot = tot + rbuf[t]
    lane = lax.broadcasted_iota(jnp.int32, (BIN_DEV, LANES), 1)
    s = tot + pltpu.roll(tot, LANES - lev, 1) + pltpu.roll(tot, LANES - 2 * lev, 1)
    count = pltpu.roll(tot, LANES - 3 * lev, 1)
    lv = pltpu.roll(s, LANES - 4 * lev, 1) / ((members - 1) * cols * ntile)
    bc = s / jnp.maximum(count, 1.0)
    w = jnp.where(lane < lev, lv * bc, 0.0)
    w = w + jnp.where((lane >= lev) & (lane < 2 * lev), pltpu.roll(lv, lev, 1), 0.0)
    lsend[...] = w
    lrecv[my_lev] = w

    def l_copy(d):
        peer = lax.rem(my_lev + d, nlev)
        return pltpu.make_async_remote_copy(
            src_ref=lsend, dst_ref=lrecv.at[my_lev],
            send_sem=l_send.at[d], recv_sem=l_recv.at[my_lev],
            device_id=(me, peer), device_id_type=pl.DeviceIdType.MESH,
        )

    for d in range(1, nlev):
        l_copy(d).start()
    lv_out[...] = lv[0:1, :lev]
    corr_out[...] = jnp.transpose(bc)[:lev, :]
    for d in range(1, nlev):
        src = lax.rem(my_lev + d, nlev)
        pltpu.make_async_copy(lrecv.at[src], lrecv.at[src], l_recv.at[src]).wait()
    all_w = lrecv[0]
    for t in range(1, nlev):
        all_w = all_w + lrecv[t]
    wt = jnp.transpose(all_w)
    num = jnp.sum(wt[:lev], axis=0, keepdims=True)
    den = jnp.sum(wt[lev:2 * lev], axis=0, keepdims=True)
    avg_out[...] = num / den

    for c in halos:
        c.wait_send()
    for d in range(1, ntile):
        t_copy(d).wait_send()
    for d in range(1, nlev):
        l_copy(d).wait_send()


def local(ntile, nlev, ensemble, pair_first, pair_second, pair_bin):
    members, lev, cols = ensemble.shape
    npairs = pair_first.shape[0]
    rows = members * lev
    half = cols // HALO_CHUNKS
    chunks = npairs // PAIR_CHUNK
    total_bins = BIN_DEV * ntile
    f32, bf16 = jnp.float32, jnp.bfloat16
    idx = [x.reshape(npairs // LANES, LANES) for x in (pair_first, pair_second, pair_bin)]
    vmem = pl.BlockSpec(memory_space=pltpu.VMEM)
    hbm = pl.BlockSpec(memory_space=pl.ANY)
    lv, corr, avg = pl.pallas_call(
        functools.partial(kernel, ntile, nlev),
        out_shape=(
            jax.ShapeDtypeStruct((1, lev), f32),
            jax.ShapeDtypeStruct((lev, BIN_DEV), f32),
            jax.ShapeDtypeStruct((1, BIN_DEV), f32),
        ),
        in_specs=[hbm] * 4,
        out_specs=(vmem, vmem, vmem),
        scratch_shapes=[
            pltpu.VMEM((members, lev, cols), bf16),
            pltpu.VMEM((HALO_CHUNKS, members, lev, half), bf16),
            *[pltpu.VMEM((npairs // LANES, LANES), jnp.int32)] * 3,
            pltpu.VMEM((rows + 2 * lev, cols), bf16),
            pltpu.VMEM((HALO_CHUNKS, rows + 2 * lev, half), bf16),
            pltpu.VMEM((lev, cols), f32),
            pltpu.VMEM((chunks, rows, PAIR_CHUNK), f32),
            *[pltpu.VMEM((chunks, lev, PAIR_CHUNK), f32)] * 3,
            pltpu.VMEM((total_bins, LANES), f32),
            pltpu.VMEM((ntile, BIN_DEV, LANES), f32),
            pltpu.VMEM((ntile, BIN_DEV, LANES), f32),
            pltpu.VMEM((BIN_DEV, LANES), f32),
            pltpu.VMEM((nlev, BIN_DEV, LANES), f32),
            pltpu.SemaphoreType.DMA((4,)),
            pltpu.SemaphoreType.DMA((HALO_CHUNKS,)),
            pltpu.SemaphoreType.DMA((HALO_CHUNKS,)),
            pltpu.SemaphoreType.DMA((ntile,)),
            pltpu.SemaphoreType.DMA((ntile,)),
            pltpu.SemaphoreType.DMA((nlev,)),
            pltpu.SemaphoreType.DMA((nlev,)),
        ],
        compiler_params=pltpu.CompilerParams(
            collective_id=0, has_side_effects=True, vmem_limit_bytes=60 * 1024 * 1024
        ),
        name="binned_corr",
    )(ensemble, *idx)
    return lv.reshape(lev), corr, avg.reshape(BIN_DEV)


def solution(mesh):
    in_specs = (P(None, "lev", "tile"), P("tile"), P("tile"), P("tile"))
    out_specs = (P("lev"), P("lev", "tile"), P("tile"))
    body = functools.partial(local, mesh.shape["tile"], mesh.shape["lev"])
    return jax.shard_map(body, mesh=mesh, in_specs=in_specs, out_specs=out_specs, check_vma=False)
```

time: 164 us -> 38.5 us (0.23)
  local copies, waits for them, and re-layouts: 76 us -> 2.22 us
  other arithmetic: 38.9 us -> 0 us
  Pallas kernels: 0 us -> 35.4 us
  blocking collectives: 28.9 us -> 0 us
  waiting for transfers between devices: 11.8 us -> 0 us
  starting transfers between devices: 6.03 us -> 0 us
    gather x4 -> x0, local copies, waits for them, and re-layouts: 37.3 us -> none  [the longest x2 18.7 us: accumulate(): jnp.take(extended, second, axis=0).astype(jnp.float32)]
    mul x6 -> x0, local copies, waits for them, and re-layouts: 35.8 us -> none  [the longest x2 12.1 us: accumulate(): cov = jnp.sum(left * right, axis=1) / (members - 1)]
    pallas_call x0 -> x1, Pallas kernels: none -> 35.4 us  [local(): pl.pallas_call(functools.partial(kernel, ntile, nlev), out_shape=(jax.Sha...]
    psum x2 -> x0, blocking collectives: 28.9 us -> none  [the longest x1 22.5 us: local(): lax.psum((sums, counts, own_squares), 'tile')]
    reduce_sum x11 -> x0, other arithmetic: 19.4 us -> none  [the longest x2 5.52 us: accumulate(): jnp.sum(right * right, axis=1) / (members - 1) + 1e-06]
    mul x2 -> x0, other arithmetic: 15.9 us -> none  [accumulate(): cov = jnp.sum(left * right, axis=1) / (members - 1)]
    ppermute x1 -> x0, waiting for transfers between devices: 11.8 us -> none  [from_behind(): return lax.ppermute(block, axis, route)]
    ppermute x1 -> x0, starting transfers between devices: 6.03 us -> none  [from_behind(): return lax.ppermute(block, axis, route)]
  transfers between devices with their start and end apart: 1 -> 0, of which waited for: 1 -> 0; matrix products, arithmetic and copies ran while one was open for 1% -> 0% of each run, Pallas kernels for 0% -> 0%
where the time goes in v1:
time: 38.5 us; the launch traced here: 38.3 us
  Pallas kernels  35.4 us (92%)
  local copies, waits for them, and re-layouts  2.22 us (6%)
  between operations  0.66 us (2%)
    pallas_call x1, Pallas kernels, local(): pl.pallas_call(functools.partial(kernel, ntile, nlev), out_shape=(jax.Sha...  35.4 us
    unnamed x9, local copies, waits for them, and re-layouts  2.22 us

profile of v1, /device:TPU:0, one launch (start us, length us, event | category | flops | bytes accessed | tf_op | source)
XLA Modules:
  0.0 38.3 jit_solution(5597307696226461113)
XLA Ops:
  0.6 35.4 %binned_corr.1 = (f32[1,8]{1,0:T(1,128)}, f32[8,8]{1,0:T(8,128)}, f32[1,8]{1,0:T(1,128)}) custom-call(bf16[80,8,512]{2,1,0:T(8,128)(2,1)} %ens.1, s32[32,128]{1,0:T(8,128)} %bitcast.5, s32[32,128]{1,0:T(8,128)} %bitcast.6, s32[32,128]{1,0:T(8,128)} %bitcast.7), custom_call_target="tpu_custom_call" | custom-call | tf_op jit(solution)/shard_map/binned_corr/pallas_call | solution.py:226
  36.1 0.0 copy-start
  36.1 0.0 copy-start.2
  36.1 0.6 %copy-done.2 = f32[1,8]{1,0:T(1,128)S(1)} copy-done((f32[1,8]{1,0:T(1,128)S(1)}, f32[1,8]{1,0:T(1,128)}, u32[]{:S(2)}) %copy-start.2) | copy-done | bytes 56
  36.7 0.5 %copy.10 = f32[8]{0:T(128)} copy(f32[8]{0:T(128)S(1)} %bitcast.9) | data formatting | bytes 64
  37.2 0.0 copy-done
  37.2 0.0 copy-start.1
  37.2 0.6 %copy.11 = f32[8,8]{1,0:T(8,128)} copy(f32[8,8]{1,0:T(8,128)S(1)} %copy-done) | data formatting | bytes 512
  37.8 0.0 copy-done.1
  37.8 0.5 %copy.12 = f32[8]{0:T(128)} copy(f32[8]{0:T(128)S(1)} %bitcast.8) | data formatting | bytes 64
Async XLA Ops:
  36.1 1.1 %copy-start = (f32[8,8]{1,0:T(8,128)S(1)}, f32[8,8]{1,0:T(8,128)}, u32[]{:S(2)}) copy-start(f32[8,8]{1,0:T(8,128)} %get-tuple-element.13) | copy-start | bytes 772
  36.1 0.6 %copy-start.2 = (f32[1,8]{1,0:T(1,128)S(1)}, f32[1,8]{1,0:T(1,128)}, u32[]{:S(2)}) copy-start(f32[1,8]{1,0:T(1,128)} %get-tuple-element.6) | copy-start | bytes 100
  37.2 0.6 %copy-start.1 = (f32[1,8]{1,0:T(1,128)S(1)}, f32[1,8]{1,0:T(1,128)}, u32[]{:S(2)}) copy-start(f32[1,8]{1,0:T(1,128)} %get-tuple-element.8) | copy-start | bytes 100

commit v2 on v1

--- a/solution.py
+++ b/solution.py
@@ -44,9 +44,9 @@
 
 
 def kernel(
-    ntile, nlev, ens, first_in, second_in, bin_in, lv_out, corr_out, avg_out,
+    ntile, nlev, ens, first_in, second_in, bin_in, packed,
     raw, halo, first, second, bins, own, nxt, squares, left_buf, cov_buf, ia_buf, ib_buf,
-    bacc, sbuf, rbuf, lsend, lrecv,
+    bin_hot, parts_buf, bacc, sbuf, rbuf, lsend, lrecv,
     load_sem, halo_send, halo_recv, t_send, t_recv, l_send, l_recv,
 ):
     members, lev, cols = ens.shape
@@ -115,7 +115,13 @@
         return carry
 
     lax.fori_loop(0, chunks, own_step, 0)
-    bacc[...] = jnp.zeros_like(bacc)
+    def bin_step(j, carry):
+        cs = pl.ds(pl.multiple_of(j * PAIR_CHUNK, PAIR_CHUNK), PAIR_CHUNK)
+        bin_hot[:, cs] = onehot(index_rows(bins, j), 0, total_bins)
+        return carry
+
+    lax.fori_loop(0, chunks, bin_step, 0)
+    parts_buf[...] = jnp.zeros_like(parts_buf)
 
     for h in range(HALO_CHUNKS):
         halos[h].wait_recv()
@@ -133,16 +139,16 @@
                 corr = cov * ia_buf[j] * ib / (members - 1)
                 parts = jnp.concatenate(
                     [*pieces3(corr), jnp.ones_like(corr),
-                     jnp.zeros((LANES - 4 * lev, PAIR_CHUNK), jnp.float32)], axis=0
+                     ], axis=0
                 ).astype(jnp.bfloat16)
-                oh = onehot(index_rows(bins, j), 0, total_bins)
-                bacc[...] += lax.dot_general(
-                    oh, parts, (((1,), (1,)), ((), ())), preferred_element_type=jnp.float32
-                )
+                parts_buf[pl.ds(0, 4 * lev), pl.ds(pl.multiple_of(j * PAIR_CHUNK, PAIR_CHUNK), PAIR_CHUNK)] = parts
             return carry
 
-        lax.fori_loop(0, chunks, next_step, 0)
-
+        lax.fori_loop(0, chunks, next_step, 0, unroll=4)
+
+    bacc[...] = lax.dot_general(
+        bin_hot[...], parts_buf[...], (((1,), (1,)), ((), ())), preferred_element_type=jnp.float32
+    )
     sq_parts = jnp.concatenate(
         [jnp.zeros((4 * lev, cols), jnp.float32), *pieces3(squares[...]),
          jnp.zeros((LANES - 7 * lev, cols), jnp.float32)], axis=0
@@ -191,25 +197,32 @@
 
     for d in range(1, nlev):
         l_copy(d).start()
-    lv_out[...] = lv[0:1, :lev]
-    corr_out[...] = jnp.transpose(bc)[:lev, :]
+    packed[0] = lv
+    packed[1] = bc
     for d in range(1, nlev):
         src = lax.rem(my_lev + d, nlev)
         pltpu.make_async_copy(lrecv.at[src], lrecv.at[src], l_recv.at[src]).wait()
     all_w = lrecv[0]
     for t in range(1, nlev):
         all_w = all_w + lrecv[t]
-    wt = jnp.transpose(all_w)
+    packed[2] = all_w
+
+    for c in halos:
+        c.wait_send()
+    for d in range(1, ntile):
+        t_copy(d).wait_send()
+    for d in range(1, nlev):
+        l_copy(d).wait_send()
+
+
+def unpack(packed, lv_out, corr_out, avg_out):
+    lev = corr_out.shape[0]
+    lv_out[...] = packed[0, 0:1, :lev]
+    corr_out[...] = jnp.transpose(packed[1])[:lev, :]
+    wt = jnp.transpose(packed[2])
     num = jnp.sum(wt[:lev], axis=0, keepdims=True)
     den = jnp.sum(wt[lev:2 * lev], axis=0, keepdims=True)
     avg_out[...] = num / den
-
-    for c in halos:
-        c.wait_send()
-    for d in range(1, ntile):
-        t_copy(d).wait_send()
-    for d in range(1, nlev):
-        l_copy(d).wait_send()
 
 
 def local(ntile, nlev, ensemble, pair_first, pair_second, pair_bin):
@@ -223,15 +236,11 @@
     idx = [x.reshape(npairs // LANES, LANES) for x in (pair_first, pair_second, pair_bin)]
     vmem = pl.BlockSpec(memory_space=pltpu.VMEM)
     hbm = pl.BlockSpec(memory_space=pl.ANY)
-    lv, corr, avg = pl.pallas_call(
+    packed = pl.pallas_call(
         functools.partial(kernel, ntile, nlev),
-        out_shape=(
-            jax.ShapeDtypeStruct((1, lev), f32),
-            jax.ShapeDtypeStruct((lev, BIN_DEV), f32),
-            jax.ShapeDtypeStruct((1, BIN_DEV), f32),
-        ),
+        out_shape=jax.ShapeDtypeStruct((3, BIN_DEV, LANES), f32),
         in_specs=[hbm] * 4,
-        out_specs=(vmem, vmem, vmem),
+        out_specs=vmem,
         scratch_shapes=[
             pltpu.VMEM((members, lev, cols), bf16),
             pltpu.VMEM((HALO_CHUNKS, members, lev, half), bf16),
@@ -241,6 +250,8 @@
             pltpu.VMEM((lev, cols), f32),
             pltpu.VMEM((chunks, rows, PAIR_CHUNK), f32),
             *[pltpu.VMEM((chunks, lev, PAIR_CHUNK), f32)] * 3,
+            pltpu.VMEM((total_bins, npairs), bf16),
+            pltpu.VMEM((LANES, npairs), bf16),
             pltpu.VMEM((total_bins, LANES), f32),
             pltpu.VMEM((ntile, BIN_DEV, LANES), f32),
             pltpu.VMEM((ntile, BIN_DEV, LANES), f32),
@@ -259,6 +270,17 @@
         ),
         name="binned_corr",
     )(ensemble, *idx)
+    lv, corr, avg = pl.pallas_call(
+        unpack,
+        out_shape=(
+            jax.ShapeDtypeStruct((1, lev), f32),
+            jax.ShapeDtypeStruct((lev, BIN_DEV), f32),
+            jax.ShapeDtypeStruct((1, BIN_DEV), f32),
+        ),
+        in_specs=[vmem],
+        out_specs=(vmem, vmem, vmem),
+        name="unpack",
+    )(packed)
     return lv.reshape(lev), corr, avg.reshape(BIN_DEV)
 
 

time: 38.5 us -> 35.7 us (0.927)
  local copies, waits for them, and re-layouts: 2.22 us -> 0 us
  Pallas kernels: 35.4 us -> 34.9 us
    unnamed x9 -> x0, local copies, waits for them, and re-layouts: 2.22 us -> none
    pallas_call x1 -> x2, Pallas kernels: 35.4 us -> 34.9 us  [the longest x1 33.5 us: local(): pl.pallas_call(functools.partial(kernel, ntile, nlev), out_shape=jax.Shap...]
where the time goes in v2:
time: 35.7 us; the launch traced here: 35.5 us
  Pallas kernels  34.9 us (98%)
  between operations  0.64 us (2%)
    pallas_call x1, Pallas kernels, local(): pl.pallas_call(functools.partial(kernel, ntile, nlev), out_shape=jax.Shap...  33.5 us
    pallas_call x1, Pallas kernels, local(): pl.pallas_call(unpack, out_shape=(jax.ShapeDtypeStruct((1, lev), f32), ja...  1.37 us

profile of v2, /device:TPU:0, one launch (start us, length us, event | category | flops | bytes accessed | tf_op | source)
XLA Modules:
  0.0 35.5 jit_solution(16057663572510700413)
XLA Ops:
  0.6 33.5 %binned_corr.1.packed = f32[3,8,128]{2,1,0:T(8,128)} custom-call(bf16[80,8,512]{2,1,0:T(8,128)(2,1)} %ens.1, s32[32,128]{1,0:T(8,128)} %bitcast.5, s32[32,128]{1,0:T(8,128)} %bitcast.6, s32[32,128]{1,0:T(8,128)} %bitcast.7), custom_call_target="tpu_custom_call" | custom-call | tf_op jit(solution)/shard_map/binned_corr/pallas_call | solution.py:239
  34.2 1.4 %unpack.1 = (f32[1,8]{1,0:T(1,128)}, f32[8,8]{1,0:T(8,128)}, f32[1,8]{1,0:T(1,128)}) custom-call(f32[3,8,128]{2,1,0:T(8,128)} %binned_corr.1.packed), custom_call_target="tpu_custom_call" | custom-call | tf_op jit(solution)/shard_map/unpack/pallas_call | solution.py:273

commit v3 on v2

--- a/solution.py
+++ b/solution.py
@@ -43,15 +43,27 @@
             squares[:, cs] = sq
 
 
+def spread_lanes(x, lev):
+    lane = lax.broadcasted_iota(jnp.int32, x.shape, 1)
+    s = x + pltpu.roll(x, LANES - lev, 1) + pltpu.roll(x, LANES - 2 * lev, 1)
+    s = jnp.where(lane < lev, s, 0.0)
+    width = lev
+    while width < BIN_DEV * lev:
+        s = s + pltpu.roll(s, width, 1)
+        width *= 2
+    return s
+
+
 def kernel(
     ntile, nlev, ens, first_in, second_in, bin_in, packed,
     raw, halo, first, second, bins, own, nxt, squares, left_buf, cov_buf, ia_buf, ib_buf,
-    bin_hot, parts_buf, bacc, sbuf, rbuf, lsend, lrecv,
-    load_sem, halo_send, halo_recv, t_send, t_recv, l_send, l_recv,
+    bin_hot, parts_buf, bacc, sq_buf, sbuf, rbuf,
+    load_sem, halo_send, halo_recv, x_send, x_recv, ready,
 ):
     members, lev, cols = ens.shape
     rows = members * lev
     half = cols // HALO_CHUNKS
+    npairs = bin_hot.shape[1]
     total_bins = BIN_DEV * ntile
     chunks = left_buf.shape[0]
     groups = PAIR_CHUNK // LANES
@@ -93,6 +105,11 @@
     ]
     for c in halos:
         c.start()
+    for d in range(1, nlev):
+        pl.semaphore_signal(
+            ready, inc=1, device_id=(me, lax.rem(my_lev + d, nlev)),
+            device_id_type=pl.DeviceIdType.MESH,
+        )
     for c in loads[1:]:
         c.wait()
 
@@ -121,7 +138,18 @@
         return carry
 
     lax.fori_loop(0, chunks, bin_step, 0)
-    parts_buf[...] = jnp.zeros_like(parts_buf)
+    parts_buf[...] = jnp.concatenate(
+        [jnp.zeros((BIN_DEV * lev, npairs), jnp.float32), jnp.ones((LANES - BIN_DEV * lev, npairs), jnp.float32)], axis=0
+    ).astype(jnp.bfloat16)
+    sq_parts = jnp.concatenate(
+        [*pieces3(squares[...]), jnp.zeros((LANES - 3 * lev, cols), jnp.float32)], axis=0
+    ).astype(jnp.bfloat16)
+    sq_row = lax.dot_general(
+        jnp.ones((16, cols), jnp.bfloat16), sq_parts, (((1,), (1,)), ((), ())),
+        preferred_element_type=jnp.float32,
+    )[:BIN_DEV]
+    sq_buf[...] = spread_lanes(sq_row, lev)
+    pl.semaphore_wait(ready, nlev - 1)
 
     for h in range(HALO_CHUNKS):
         halos[h].wait_recv()
@@ -138,8 +166,7 @@
             else:
                 corr = cov * ia_buf[j] * ib / (members - 1)
                 parts = jnp.concatenate(
-                    [*pieces3(corr), jnp.ones_like(corr),
-                     ], axis=0
+                    [*pieces3(corr), jnp.zeros_like(corr)], axis=0
                 ).astype(jnp.bfloat16)
                 parts_buf[pl.ds(0, 4 * lev), pl.ds(pl.multiple_of(j * PAIR_CHUNK, PAIR_CHUNK), PAIR_CHUNK)] = parts
             return carry
@@ -149,79 +176,81 @@
     bacc[...] = lax.dot_general(
         bin_hot[...], parts_buf[...], (((1,), (1,)), ((), ())), preferred_element_type=jnp.float32
     )
-    sq_parts = jnp.concatenate(
-        [jnp.zeros((4 * lev, cols), jnp.float32), *pieces3(squares[...]),
-         jnp.zeros((LANES - 7 * lev, cols), jnp.float32)], axis=0
-    ).astype(jnp.bfloat16)
-    sq_row = lax.dot_general(
-        jnp.ones((16, cols), jnp.bfloat16), sq_parts, (((1,), (1,)), ((), ())),
-        preferred_element_type=jnp.float32,
-    )[:BIN_DEV]
+    half_lanes = BIN_DEV * lev
+    wide_lane = lax.broadcasted_iota(jnp.int32, (total_bins, LANES), 1)
+    wide = jnp.where(wide_lane < half_lanes, spread_lanes(bacc[...], lev), bacc[...])
+    lane = lax.broadcasted_iota(jnp.int32, (BIN_DEV, LANES), 1)
+    bin_row = lax.broadcasted_iota(jnp.int32, (BIN_DEV, LANES), 0)
+    pick = (lax.rem(lane, half_lanes) // lev == bin_row).astype(jnp.float32)
     for t in range(ntile):
-        sbuf[t] = bacc[pl.ds(t * BIN_DEV, BIN_DEV), :] + sq_row
-    rbuf[me] = sbuf[me]
-
-    def t_copy(d):
-        peer = lax.rem(me + d, ntile)
+        block = wide[t * BIN_DEV:(t + 1) * BIN_DEV] * pick
+        sbuf[t, 0:1, :] = jnp.sum(block, axis=0, keepdims=True)
+        sbuf[t, 1:2, :] = sq_buf[0:1, :]
+    mine = my_lev * ntile + me
+    rbuf[mine] = sbuf[me]
+
+    def x_copy(d):
+        dl, dt = d // ntile, d % ntile
+        peer_t = lax.rem(me + dt, ntile)
+        peer_l = lax.rem(my_lev + dl, nlev)
         return pltpu.make_async_remote_copy(
-            src_ref=sbuf.at[peer], dst_ref=rbuf.at[me],
-            send_sem=t_send.at[d], recv_sem=t_recv.at[me],
-            device_id=(peer, my_lev), device_id_type=pl.DeviceIdType.MESH,
-        )
-
-    for d in range(1, ntile):
-        t_copy(d).start()
-    for d in range(1, ntile):
-        src = lax.rem(me + d, ntile)
-        pltpu.make_async_copy(rbuf.at[src], rbuf.at[src], t_recv.at[src]).wait()
-    tot = rbuf[0]
-    for t in range(1, ntile):
-        tot = tot + rbuf[t]
-    lane = lax.broadcasted_iota(jnp.int32, (BIN_DEV, LANES), 1)
-    s = tot + pltpu.roll(tot, LANES - lev, 1) + pltpu.roll(tot, LANES - 2 * lev, 1)
-    count = pltpu.roll(tot, LANES - 3 * lev, 1)
-    lv = pltpu.roll(s, LANES - 4 * lev, 1) / ((members - 1) * cols * ntile)
-    bc = s / jnp.maximum(count, 1.0)
-    w = jnp.where(lane < lev, lv * bc, 0.0)
-    w = w + jnp.where((lane >= lev) & (lane < 2 * lev), pltpu.roll(lv, lev, 1), 0.0)
-    lsend[...] = w
-    lrecv[my_lev] = w
-
-    def l_copy(d):
-        peer = lax.rem(my_lev + d, nlev)
-        return pltpu.make_async_remote_copy(
-            src_ref=lsend, dst_ref=lrecv.at[my_lev],
-            send_sem=l_send.at[d], recv_sem=l_recv.at[my_lev],
-            device_id=(me, peer), device_id_type=pl.DeviceIdType.MESH,
-        )
-
-    for d in range(1, nlev):
-        l_copy(d).start()
-    packed[0] = lv
-    packed[1] = bc
-    for d in range(1, nlev):
-        src = lax.rem(my_lev + d, nlev)
-        pltpu.make_async_copy(lrecv.at[src], lrecv.at[src], l_recv.at[src]).wait()
-    all_w = lrecv[0]
-    for t in range(1, nlev):
-        all_w = all_w + lrecv[t]
-    packed[2] = all_w
+            src_ref=sbuf.at[peer_t], dst_ref=rbuf.at[mine],
+            send_sem=x_send.at[d], recv_sem=x_recv.at[mine],
+            device_id=(peer_t, peer_l), device_id_type=pl.DeviceIdType.MESH,
+        )
+
+    def x_start(d, carry):
+        x_copy(d).start()
+        return carry
+
+    def x_wait_send(d, carry):
+        x_copy(d).wait_send()
+        return carry
+
+    def x_wait(d, carry):
+        src = lax.rem(my_lev + d // ntile, nlev) * ntile + lax.rem(me + d % ntile, ntile)
+        pltpu.make_async_copy(rbuf.at[src], rbuf.at[src], x_recv.at[src]).wait()
+        return carry
+
+    everyone = ntile * nlev
+    small = everyone <= 64
+    lax.fori_loop(1, everyone, x_start, 0, unroll=small)
+    lax.fori_loop(1, everyone, x_wait, 0, unroll=small)
+    num = jnp.zeros((1, LANES), jnp.float32)
+    den = num
+    own_lv = num
+    own_bc = num
+    for v in range(nlev):
+        tot = rbuf[v * ntile]
+        for t in range(1, ntile):
+            tot = tot + rbuf[v * ntile + t]
+        sums, lv = tot[0:1], tot[1:2] / ((members - 1) * cols * ntile)
+        bc = sums / jnp.maximum(pltpu.roll(sums, LANES - half_lanes, 1), 1.0)
+        num = num + lv * bc
+        den = den + lv
+        own_lv = jnp.where(my_lev == v, lv, own_lv)
+        own_bc = jnp.where(my_lev == v, bc, own_bc)
+    for i, row in enumerate((own_lv, own_bc, num, den)):
+        packed[i:i + 1, :] = row
 
     for c in halos:
         c.wait_send()
-    for d in range(1, ntile):
-        t_copy(d).wait_send()
-    for d in range(1, nlev):
-        l_copy(d).wait_send()
+    lax.fori_loop(1, everyone, x_wait_send, 0, unroll=small)
 
 
 def unpack(packed, lv_out, corr_out, avg_out):
     lev = corr_out.shape[0]
-    lv_out[...] = packed[0, 0:1, :lev]
-    corr_out[...] = jnp.transpose(packed[1])[:lev, :]
-    wt = jnp.transpose(packed[2])
-    num = jnp.sum(wt[:lev], axis=0, keepdims=True)
-    den = jnp.sum(wt[lev:2 * lev], axis=0, keepdims=True)
+    lane = lax.broadcasted_iota(jnp.int32, (BIN_DEV, LANES), 1)
+    bin_row = lax.broadcasted_iota(jnp.int32, (BIN_DEV, LANES), 0)
+
+    def by_bin(row):
+        x = jnp.where(lane // lev == bin_row, row, 0.0)
+        return jnp.sum(jnp.transpose(x).reshape(LANES // lev, lev, BIN_DEV), axis=0)
+
+    lv_out[...] = packed[0:1, :lev]
+    corr_out[...] = by_bin(packed[1:2, :])
+    num = jnp.sum(by_bin(packed[2:3, :]), axis=0, keepdims=True)
+    den = jnp.sum(by_bin(packed[3:4, :]), axis=0, keepdims=True)
     avg_out[...] = num / den
 
 
@@ -238,7 +267,7 @@
     hbm = pl.BlockSpec(memory_space=pl.ANY)
     packed = pl.pallas_call(
         functools.partial(kernel, ntile, nlev),
-        out_shape=jax.ShapeDtypeStruct((3, BIN_DEV, LANES), f32),
+        out_shape=jax.ShapeDtypeStruct((8, LANES), f32),
         in_specs=[hbm] * 4,
         out_specs=vmem,
         scratch_shapes=[
@@ -253,17 +282,15 @@
             pltpu.VMEM((total_bins, npairs), bf16),
             pltpu.VMEM((LANES, npairs), bf16),
             pltpu.VMEM((total_bins, LANES), f32),
-            pltpu.VMEM((ntile, BIN_DEV, LANES), f32),
-            pltpu.VMEM((ntile, BIN_DEV, LANES), f32),
             pltpu.VMEM((BIN_DEV, LANES), f32),
-            pltpu.VMEM((nlev, BIN_DEV, LANES), f32),
+            pltpu.VMEM((ntile, 2, LANES), f32),
+            pltpu.VMEM((nlev * ntile, 2, LANES), f32),
             pltpu.SemaphoreType.DMA((4,)),
             pltpu.SemaphoreType.DMA((HALO_CHUNKS,)),
             pltpu.SemaphoreType.DMA((HALO_CHUNKS,)),
-            pltpu.SemaphoreType.DMA((ntile,)),
-            pltpu.SemaphoreType.DMA((ntile,)),
-            pltpu.SemaphoreType.DMA((nlev,)),
-            pltpu.SemaphoreType.DMA((nlev,)),
+            pltpu.SemaphoreType.DMA((nlev * ntile,)),
+            pltpu.SemaphoreType.DMA((nlev * ntile,)),
+            pltpu.SemaphoreType.REGULAR,
         ],
         compiler_params=pltpu.CompilerParams(
             collective_id=0, has_side_effects=True, vmem_limit_bytes=60 * 1024 * 1024

time: 35.7 us -> 34.2 us (0.958)
  Pallas kernels: 34.9 us -> 33.4 us
    pallas_call x1, Pallas kernels: 33.5 us -> 32 us  [local(): pl.pallas_call(functools.partial(kernel, ntile, nlev), out_shape=jax.Shap...]
where the time goes in v3:
time: 34.2 us; the launch traced here: 34 us
  Pallas kernels  33.4 us (98%)
  between operations  0.64 us (2%)
    pallas_call x1, Pallas kernels, local(): pl.pallas_call(functools.partial(kernel, ntile, nlev), out_shape=jax.Shap...  32 us
    pallas_call x1, Pallas kernels, local(): pl.pallas_call(unpack, out_shape=(jax.ShapeDtypeStruct((1, lev), f32), ja...  1.37 us

profile of v3, /device:TPU:0, one launch (start us, length us, event | category | flops | bytes accessed | tf_op | source)
XLA Modules:
  0.0 34.0 jit_solution(2928482177010728050)
XLA Ops:
  0.6 32.0 %binned_corr.1.packed = f32[8,128]{1,0:T(8,128)} custom-call(bf16[80,8,512]{2,1,0:T(8,128)(2,1)} %ens.1, s32[32,128]{1,0:T(8,128)} %bitcast.5, s32[32,128]{1,0:T(8,128)} %bitcast.6, s32[32,128]{1,0:T(8,128)} %bitcast.7), custom_call_target="tpu_custom_call" | custom-call | tf_op jit(solution)/shard_map/binned_corr/pallas_call | solution.py:268
  32.6 1.4 %unpack.1 = (f32[1,8]{1,0:T(1,128)}, f32[8,8]{1,0:T(8,128)}, f32[1,8]{1,0:T(1,128)}) custom-call(f32[8,128]{1,0:T(8,128)} %binned_corr.1.packed), custom_call_target="tpu_custom_call" | custom-call | tf_op jit(solution)/shard_map/unpack/pallas_call | solution.py:300

commit v4 on v3

--- a/solution.py
+++ b/solution.py
@@ -171,7 +171,7 @@
                 parts_buf[pl.ds(0, 4 * lev), pl.ds(pl.multiple_of(j * PAIR_CHUNK, PAIR_CHUNK), PAIR_CHUNK)] = parts
             return carry
 
-        lax.fori_loop(0, chunks, next_step, 0, unroll=4)
+        lax.fori_loop(0, chunks, next_step, 0, unroll=8)
 
     bacc[...] = lax.dot_general(
         bin_hot[...], parts_buf[...], (((1,), (1,)), ((), ())), preferred_element_type=jnp.float32

time: 34.2 us -> 33.9 us (level)
  no operation moved by 1% of the time
where the time goes in v4:
time: 33.9 us; the launch traced here: 33.7 us
  Pallas kernels  33.1 us (98%)
  between operations  0.64 us (2%)
    pallas_call x1, Pallas kernels, local(): pl.pallas_call(functools.partial(kernel, ntile, nlev), out_shape=jax.Shap...  31.7 us
    pallas_call x1, Pallas kernels, local(): pl.pallas_call(unpack, out_shape=(jax.ShapeDtypeStruct((1, lev), f32), ja...  1.37 us

profile of v4, /device:TPU:0, one launch (start us, length us, event | category | flops | bytes accessed | tf_op | source)
XLA Modules:
  0.0 33.7 jit_solution(8867087564475353142)
XLA Ops:
  0.6 31.7 %binned_corr.1.packed = f32[8,128]{1,0:T(8,128)} custom-call(bf16[80,8,512]{2,1,0:T(8,128)(2,1)} %ens.1, s32[32,128]{1,0:T(8,128)} %bitcast.5, s32[32,128]{1,0:T(8,128)} %bitcast.6, s32[32,128]{1,0:T(8,128)} %bitcast.7), custom_call_target="tpu_custom_call" | custom-call | tf_op jit(solution)/shard_map/binned_corr/pallas_call | solution.py:268
  32.4 1.4 %unpack.1 = (f32[1,8]{1,0:T(1,128)}, f32[8,8]{1,0:T(8,128)}, f32[1,8]{1,0:T(1,128)}) custom-call(f32[8,128]{1,0:T(8,128)} %binned_corr.1.packed), custom_call_target="tpu_custom_call" | custom-call | tf_op jit(solution)/shard_map/unpack/pallas_call | solution.py:300
